TPU v7x, 128 devices: a whole 4x4x4 slice. The times are simulated.
128 devices in a mesh: walk: 8 (over y, z_hi), chol: 16 (over z_lo, x, core).
Axes of the slice: x: 4, y: 4, z: 4 (z_hi: 2, z_lo: 2; z = z_hi * 2 + z_lo), core: 2. Of those that a mesh axis runs over, the one named last changes fastest.
Arguments:
- orbitals: bfloat16 [1024, 64, 1024], P(('walk', 'chol')), may hold values from -6 to 6
- cholesky: bfloat16 [192, 64, 1024], P('chol'), may hold values from -0.1875 to 0.1875
- parents: int32 [1024], P(('walk', 'chol')), may hold values from 0 to 1023, as said below
- counts: int32 [8, 16], P('walk', 'chol'), may hold values from 1 to 8, as said below
- steps: bfloat16 [1024, 64, 1024], P(('walk', 'chol')), may hold values from -6 to 6
Outputs:
- energy: float32 [1024], P(('walk', 'chol'))
- parent_grad: float32 [1024, 64, 1024], P(('walk', 'chol'))
Inputs may be any that keep to these rules, and one draw needn't show every extreme that they name: The parent of a new walker lies on the same index of chol as the walker. Of one device's new walkers at most 2 have parents on any one index of walk, and on some index exactly 2. The first counts entries of a device's 8 new walkers are live; in every draw some device is full.
All inputs are finite; a program needn't handle non-finite values.
Results may differ from a plain program's by a relative error of at most 0.0044.
Values may be sent and summed in bfloat16 or wider, within the bound.
A program may use at most 128 MiB of HBM per device.

v0:
```python
import jax
import jax.numpy as jnp
from jax import lax
from jax.sharding import Mesh
from jax.sharding import PartitionSpec as P

CAP = 2
WALK = ("walk_0", "walk_1")
WALK_CHOL = ("walk_0", "walk_1", "chol")


def cut_along(shard, dim, devices):
    before, after = (shard.shape[:dim], shard.shape[dim + 1 :])
    return jnp.moveaxis(shard.reshape(*before, devices, -1, *after), dim, 0)


def in_order(parts, dim):
    shape = list(parts.shape[1:])
    shape[dim] *= parts.shape[0]
    return jnp.moveaxis(parts, 0, dim).reshape(shape)


def turned_blocks(parts, axes, sequence):
    shape = [lax.axis_size(a) for a in axes]
    parts = parts.reshape(*shape, *parts.shape[1:])
    for k in sequence:
        parts = lax.all_to_all(parts, axes[k], split_axis=k, concat_axis=k, tiled=True)
    return parts.reshape(-1, *parts.shape[len(axes) :])


def one_axis_at_a_time(shard, axes, sequence, split_dim, concat_dim):
    parts = cut_along(shard, split_dim, lax.axis_size(axes))
    return in_order(turned_blocks(parts, axes, sequence), concat_dim)


def body(orbitals, cholesky, parents, counts, steps):
    walk_size = lax.axis_size(WALK)
    chol_size = lax.axis_size("chol")
    per_device = orbitals.shape[0]
    electrons = orbitals.shape[1]
    basis_len = orbitals.shape[2]
    vectors_dev = cholesky.shape[0]
    source_walk = parents // (chol_size * per_device)
    source_slot = parents % per_device
    position = jnp.arange(per_device, dtype=jnp.int32)
    earlier_same = (source_walk[:, None] == source_walk[None, :]) & (
        position[None, :] < position[:, None]
    )
    rank_within = jnp.sum(earlier_same.astype(jnp.int32), axis=1)
    slot_ids = source_walk * CAP + rank_within
    flat_slots = jnp.arange(walk_size * CAP, dtype=jnp.int32)
    matching = slot_ids[:, None] == flat_slots[None, :]
    wanted = jnp.sum(matching.astype(jnp.int32) * (source_slot[:, None] + 1), axis=0) - 1
    asked = one_axis_at_a_time(wanted.reshape(walk_size, CAP), WALK, (0, 1), 0, 0).reshape(-1)
    picker = (asked[:, None] == position[None, :]).astype(jnp.bfloat16)
    outgoing = jnp.dot(picker, orbitals.reshape(per_device, -1), preferred_element_type=jnp.float32)
    outgoing = outgoing.astype(jnp.bfloat16).reshape(walk_size, CAP, electrons, basis_len)
    incoming = lax.all_to_all(outgoing, WALK, split_axis=0, concat_axis=0, tiled=True)
    gathered = jnp.dot(
        matching.astype(jnp.bfloat16),
        incoming.reshape(walk_size * CAP, -1),
        preferred_element_type=jnp.float32,
    )
    clones = gathered + steps.reshape(per_device, -1).astype(jnp.float32)
    clones = clones.astype(jnp.bfloat16).reshape(per_device, electrons, basis_len)
    piece = lax.all_gather(cholesky, "chol", axis=0, tiled=True)
    shards = piece.shape[0] // vectors_dev
    blocks = piece.reshape(shards, vectors_dev, electrons, basis_len)
    intersection = jnp.einsum(
        "sgip,wjp->swgij", blocks, clones, preferred_element_type=jnp.float32
    ).astype(jnp.bfloat16)
    part = -jnp.einsum("swgji,sgip->swjp", intersection, blocks, preferred_element_type=jnp.float32)
    part = lax.optimization_barrier(part.astype(jnp.bfloat16))
    gradient = jnp.sum(part.astype(jnp.float32), axis=0)
    alive = (position < counts.reshape(-1)[0]).astype(jnp.float32)
    gradient = gradient * alive[:, None, None]
    energy = 0.5 * jnp.sum(clones.astype(jnp.float32) * gradient, axis=(1, 2))
    backward = jnp.dot(
        matching.T.astype(jnp.float32),
        gradient.reshape(per_device, -1),
        precision=lax.Precision.HIGHEST,
    )
    backward = backward.reshape(walk_size, CAP, electrons, basis_len)
    returned = lax.all_to_all(backward, WALK, split_axis=0, concat_axis=0, tiled=True)
    owner = (asked[None, :] == position[:, None]).astype(jnp.float32)
    parent_grad = jnp.dot(
        owner, returned.reshape(walk_size * CAP, -1), precision=lax.Precision.HIGHEST
    )
    return (energy, parent_grad.reshape(per_device, electrons, basis_len))


def solution(mesh):
    torus = Mesh(mesh.devices.reshape(4, 2, mesh.shape["chol"]), ("walk_0", "walk_1", "chol"))
    return jax.shard_map(
        body,
        mesh=torus,
        in_specs=(
            P(WALK_CHOL, None, None),
            P("chol", None, None),
            P(WALK_CHOL),
            P(WALK, "chol"),
            P(WALK_CHOL, None, None),
        ),
        out_specs=(P(WALK_CHOL), P(WALK_CHOL, None, None)),
        check_vma=False,
    )
```

profile of v0, /device:TPU:0, one launch (start us, length us, event | category | flops | bytes accessed | tf_op | source)
XLA Modules:
  0.0 311.1 jit_solution(2648531284516923733)
XLA Ops:
  7.2 0.7 all-gather.2.cloned.1.call-update
  7.9 0.7 and_select_fusion.1
  8.6 0.2 convert_reduce_fusion.1
  8.8 0.1 select_reduce_fusion
  8.9 0.7 sub.11
  9.5 4.6 %all-to-all-start = ((s32[4,2,1,2]{3,1,2,0:T(2,128)}), s32[4,2,1,2]{3,1,2,0:T(2,128)S(1)}, u32[]{:S(2)}, u32[]{:S(2)}) async-start(s32[4,2,1,2]{3,1,2,0:T(2,128)} %bitcast), calls=%async_computation | async-start | bytes 8192 | tf_op jit(solution)/shard_map/all_to_all | solution.py:27
  14.1 0.6 copy.35
  14.7 4.7 %all-to-all-done = s32[4,2,1,2]{3,1,2,0:T(2,128)S(1)} async-done(((s32[4,2,1,2]{3,1,2,0:T(2,128)}), s32[4,2,1,2]{3,1,2,0:T(2,128)S(1)}, u32[]{:S(2)}, u32[]{:S(2)}) %all-to-all-start) | async-done | bytes 96 | tf_op jit(solution)/shard_map/all_to_all | solution.py:27
  19.4 0.1 copy.20
  19.5 10.4 %all_to_all.20 = s32[4,2,1,2]{0,3,2,1:T(2,128)S(1)} all-to-all(s32[4,2,1,2]{0,3,2,1:T(2,128)S(1)} %copy.20), channel_id=1, replica_groups=mesh['walk_0'=4,'walk_1'=2,'chol'=16] {'walk_1'}, dimensions={1} | all-to-all | bytes 128 | tf_op jit(solution)/shard_map/all_to_all | solution.py:27
  29.9 0.1 copy.21
  30.1 0.8 convolution_convert_fusion
  30.8 2.5 copy.36
  33.4 3.7 %all-to-all-start.2 = ((bf16[8,2,64,1024]{3,2,1,0:T(8,128)(2,1)}), bf16[8,2,64,1024]{3,2,1,0:T(8,128)(2,1)S(1)}, u32[]{:S(2)}, u32[]{:S(2)}) async-start(bf16[8,2,64,1024]{3,2,1,0:T(8,128)(2,1)} %bitcast.74), calls=%async_computation.2 | async-start | bytes 4194304 | tf_op jit(solution)/shard_map/all_to_all | solution.py:58
  37.1 0.2 convert_bitcast_fusion
  37.4 2.5 copy.38
  40.6 27.5 %all-to-all-done.2 = bf16[8,2,64,1024]{3,2,1,0:T(8,128)(2,1)S(1)} async-done(((bf16[8,2,64,1024]{3,2,1,0:T(8,128)(2,1)}), bf16[8,2,64,1024]{3,2,1,0:T(8,128)(2,1)S(1)}, u32[]{:S(2)}, u32[]{:S(2)}) %all-to-all-start.2) | async-done | bytes 2097184 | tf_op jit(solution)/shard_map/all_to_all | solution.py:58
  68.1 1.2 copy.37
  69.2 0.5 copy-done
  69.7 0.5 fusion
  70.2 95.6 %all-gather.2.cloned.1.call-done = bf16[192,64,1024]{2,1,0:T(8,128)(2,1)} async-done(((bf16[12,64,1024]{2,1,0:T(8,128)(2,1)}), bf16[192,64,1024]{2,1,0:T(8,128)(2,1)}) %all-gather.2.cloned.1.call-update) | async-done | bytes 25165840 | tf_op jit(solution)/shard_map/all_gather | solution.py:66
  165.8 47.6 %fusion.1 = bf16[16,8,64,1024]{3,2,1,0:T(8,128)(2,1)} fusion(bf16[16,12,64,1024,1]{3,2,1,4,0:T(8,128)(2,1)} %bitcast.83, bf16[8,64,1024,1,1]{2,0,1,4,3:T(8,128)(2,1)S(1)} %bitcast.81), kind=kOutput, calls=%fused_computation.4 | convolution fusion | flops 25792872448 | bytes 42991616 | tf_op jit(solution)/shard_map/swgji,sgip->swjp/dot_general | solution.py:72
  213.4 7.3 %convert_reduce_fusion = f32[8,64,1024]{2,1,0:T(8,128)S(1)} fusion(bf16[16,8,64,1024]{3,2,1,0:T(8,128)(2,1)} %fusion.1), kind=kLoop, calls=%fused_computation.5 | loop fusion | flops 16252928 | bytes 18874368 | tf_op jit(solution)/shard_map/reduce_sum | solution.py:74
  220.8 1.2 copy.39
  222.0 0.9 multiply_reduce_fusion
  222.9 1.8 fusion.14
  224.8 4.4 %copy.24 = f32[8,2,64,1024]{3,2,1,0:T(8,128)} copy(f32[8,2,64,1024]{3,0,2,1:T(8,128)S(1)} %fusion.14) | data formatting | bytes 8388608 | tf_op jit(solution)/shard_map/dot_general | solution.py:78
  229.2 6.6 %all-to-all-start.3 = ((f32[8,2,64,1024]{3,2,1,0:T(8,128)}), f32[8,2,64,1024]{3,2,1,0:T(8,128)}, u32[]{:S(2)}, u32[]{:S(2)}) async-start(f32[8,2,64,1024]{3,2,1,0:T(8,128)} %copy.24), calls=%async_computation.3 | async-start | bytes 8388608 | tf_op jit(solution)/shard_map/all_to_all | solution.py:84
  235.8 0.5 broadcast_multiply_fusion.1
  236.3 59.5 %all-to-all-done.3 = f32[8,2,64,1024]{3,2,1,0:T(8,128)} async-done(((f32[8,2,64,1024]{3,2,1,0:T(8,128)}), f32[8,2,64,1024]{3,2,1,0:T(8,128)}, u32[]{:S(2)}, u32[]{:S(2)}) %all-to-all-start.3) | async-done | bytes 4194336 | tf_op jit(solution)/shard_map/all_to_all | solution.py:84
  295.8 5.9 %fusion.9 = f32[8,64,1024]{2,0,1:T(8,128)S(1)} fusion(s32[16]{0:T(128)S(1)} %eq.84, f32[2,8,64,1024]{3,2,1,0:T(8,128)} %bitcast.39), kind=kOutput, calls=%fused_computation.10 | convolution fusion | flops 100663424 | bytes 6291520 | tf_op jit(solution)/shard_map/dot_general | solution.py:86
  301.7 2.5 copy.26
  (11 shorter events, 0.2 us)
Async XLA Ops:
  7.2 7.0 %copy-start.2 = (bf16[8,64,1024]{2,1,0:T(8,128)(2,1)S(1)}, bf16[8,64,1024]{2,1,0:T(8,128)(2,1)}, u32[]{:S(2)}) copy-start(bf16[8,64,1024]{2,1,0:T(8,128)(2,1)} %param.5) | copy-start | bytes 3145732
  7.2 158.6 %all-gather.2.cloned.1.call-start = ((), (), s32[]{:S(2)}) async-start(), calls=%async_computation.4 | async-start | bytes 26738688 | tf_op jit(solution)/shard_map/all_gather | solution.py:66
  9.5 9.9 %all-to-all-start = ((s32[4,2,1,2]{3,1,2,0:T(2,128)}), s32[4,2,1,2]{3,1,2,0:T(2,128)S(1)}, u32[]{:S(2)}, u32[]{:S(2)}) async-start(s32[4,2,1,2]{3,1,2,0:T(2,128)} %bitcast), calls=%async_computation | async-start | bytes 8192 | tf_op jit(solution)/shard_map/all_to_all | solution.py:27
  33.4 3.7 %copy-start.1 = (bf16[8,64,1024]{2,1,0:T(8,128)(2,1)S(1)}, bf16[8,64,1024]{2,1,0:T(8,128)(2,1)}, u32[]{:S(2)}) copy-start(bf16[8,64,1024]{2,1,0:T(8,128)(2,1)} %param.9) | copy-start | bytes 3145732
  33.4 34.7 %all-to-all-start.2 = ((bf16[8,2,64,1024]{3,2,1,0:T(8,128)(2,1)}), bf16[8,2,64,1024]{3,2,1,0:T(8,128)(2,1)S(1)}, u32[]{:S(2)}, u32[]{:S(2)}) async-start(bf16[8,2,64,1024]{3,2,1,0:T(8,128)(2,1)} %bitcast.74), calls=%async_computation.2 | async-start | bytes 4194304 | tf_op jit(solution)/shard_map/all_to_all | solution.py:58
  68.1 1.6 copy-start
  229.2 66.6 %all-to-all-start.3 = ((f32[8,2,64,1024]{3,2,1,0:T(8,128)}), f32[8,2,64,1024]{3,2,1,0:T(8,128)}, u32[]{:S(2)}, u32[]{:S(2)}) async-start(f32[8,2,64,1024]{3,2,1,0:T(8,128)} %copy.24), calls=%async_computation.3 | async-start | bytes 8388608 | tf_op jit(solution)/shard_map/all_to_all | solution.py:84
Sparse Core Ops, SparseCore 0:
  9.7 156.0 all-gather.1
where the time goes:
time: 312 us; the launch traced here: 311 us
  waiting for transfers between devices  188 us (60%)
  matrix products  56.6 us (18%)
  local copies, waits for them, and re-layouts  16.4 us (5%)
  starting transfers between devices  14.9 us (5%)
  between operations  14.8 us (5%)
  blocking collectives  10.4 us (3%)
  other arithmetic  9.99 us (3%)
    all_gather x1, waiting for transfers between devices, body(): piece = lax.all_gather(cholesky, 'chol', axis=0, tiled=True)  95.6 us
    all_to_all x1, waiting for transfers between devices, body(): lax.all_to_all(backward, WALK, split_axis=0, concat_axis=0, tiled=True)  59.5 us
    dot_general x1, matrix products, body(): jnp.einsum('swgji,sgip->swjp', intersection, blocks, preferred_element_ty...  47.6 us
    all_to_all x1, waiting for transfers between devices, body(): lax.all_to_all(outgoing, WALK, split_axis=0, concat_axis=0, tiled=True)  27.5 us
    unnamed x12, local copies, waits for them, and re-layouts  11 us
    all_to_all x1, blocking collectives, turned_blocks(): lax.all_to_all(parts, axes[k], split_axis=k, concat_axis=k, tiled=True)  10.4 us
    reduce_sum x1, other arithmetic, body(): gradient = jnp.sum(part.astype(jnp.float32), axis=0)  7.34 us
    all_to_all x1, starting transfers between devices, body(): lax.all_to_all(backward, WALK, split_axis=0, concat_axis=0, tiled=True)  6.59 us
  transfers between devices with their start and end apart: 4, of which 4 were waited for; matrix products, arithmetic and copies ran while one was open for 3% of the time, Pallas kernels for 0%

commit v1 on v0

--- a/solution.py
+++ b/solution.py
@@ -3,6 +3,7 @@
 from jax import lax
 from jax.sharding import Mesh
 from jax.sharding import PartitionSpec as P
+from jax.lax import all_to_all, axis_size
 
 CAP = 2
 WALK = ("walk_0", "walk_1")
@@ -63,7 +64,15 @@
     )
     clones = gathered + steps.reshape(per_device, -1).astype(jnp.float32)
     clones = clones.astype(jnp.bfloat16).reshape(per_device, electrons, basis_len)
-    piece = lax.all_gather(cholesky, "chol", axis=0, tiled=True)
+    piece = jnp.concatenate(
+        all_to_all(
+            jnp.stack([cholesky] * axis_size("chol"), axis=0),
+            axis_name="chol",
+            split_axis=0,
+            concat_axis=0,
+        ),
+        axis=0,
+    )
     shards = piece.shape[0] // vectors_dev
     blocks = piece.reshape(shards, vectors_dev, electrons, basis_len)
     intersection = jnp.einsum(

time: 312 us -> 541 us (1.73)
  waiting for transfers between devices: 188 us -> 395 us
  blocking collectives: 10.4 us -> 38.3 us
  between operations: 14.8 us -> 1.4 us
  local copies, waits for them, and re-layouts: 16.4 us -> 23 us
    all_to_all x1, waiting for transfers between devices: 27.5 us -> 333 us  [body(): all_to_all(jnp.stack([cholesky] * axis_size('chol'), axis=0), axis_name='...]
    all_gather x1 -> x0, waiting for transfers between devices: 95.6 us -> none  [body(): piece = lax.all_gather(cholesky, 'chol', axis=0, tiled=True)]
    all_to_all x0 -> x1, blocking collectives: none -> 28.1 us  [body(): lax.all_to_all(outgoing, WALK, split_axis=0, concat_axis=0, tiled=True)]
    another operation x0 -> x1, local copies, waits for them, and re-layouts: none -> 8.55 us  [body(): jnp.stack([cholesky] * axis_size('chol'), axis=0)]
    unnamed x12 -> x10, local copies, waits for them, and re-layouts: 11 us -> 9.09 us
  transfers between devices with their start and end apart: 4 -> 3, of which waited for: 4 -> 3; matrix products, arithmetic and copies ran while one was open for 3% -> 1% of each run, Pallas kernels for 0% -> 0%
where the time goes in v1:
time: 541 us; the launch traced here: 540 us
  waiting for transfers between devices  395 us (73%)
  matrix products  56.7 us (10%)
  blocking collectives  38.3 us (7%)
  local copies, waits for them, and re-layouts  23 us (4%)
  starting transfers between devices  14.8 us (3%)
  other arithmetic  9.99 us (2%)
    all_to_all x1, waiting for transfers between devices, body(): all_to_all(jnp.stack([cholesky] * axis_size('chol'), axis=0), axis_name='...  333 us
    all_to_all x1, waiting for transfers between devices, body(): lax.all_to_all(backward, WALK, split_axis=0, concat_axis=0, tiled=True)  59.3 us
    dot_general x1, matrix products, body(): jnp.einsum('swgji,sgip->swjp', intersection, blocks, preferred_element_ty...  47.7 us
    all_to_all x1, blocking collectives, body(): lax.all_to_all(outgoing, WALK, split_axis=0, concat_axis=0, tiled=True)  28.1 us
  transfers between devices with their start and end apart: 3, of which 3 were waited for; matrix products, arithmetic and copies ran while one was open for 1% of the time, Pallas kernels for 0%

profile of v1, /device:TPU:0, one launch (start us, length us, event | category | flops | bytes accessed | tf_op | source)
XLA Modules:
  0.0 539.6 jit_solution(16381691002898503188)
XLA Ops:
  0.6 0.7 and_select_fusion.1
  1.3 0.2 convert_reduce_fusion.1
  1.5 0.1 select_reduce_fusion
  1.6 0.7 sub.11
  2.3 4.6 all-to-all-start
  6.8 1.8 copy.35
  8.6 3.5 all-to-all-done
  12.1 0.1 copy.20
  12.2 10.2 %all_to_all.25 = s32[4,2,1,2]{0,3,2,1:T(2,128)S(1)} all-to-all(s32[4,2,1,2]{0,3,2,1:T(2,128)S(1)} %copy.20), channel_id=1, replica_groups=mesh['walk_0'=4,'walk_1'=2,'chol'=16] {'walk_1'}, dimensions={1} | all-to-all | bytes 128 | tf_op jit(solution)/shard_map/all_to_all | solution.py:28
  22.5 0.1 copy.21
  22.6 0.1 eq.84
  22.6 0.8 convolution_convert_fusion
  23.4 1.2 copy.36
  24.6 28.1 %all_to_all.26 = bf16[8,2,64,1024]{3,2,1,0:T(8,128)(2,1)S(1)} all-to-all(bf16[8,2,64,1024]{3,2,1,0:T(8,128)(2,1)S(1)} %bitcast.85), channel_id=1, replica_groups=mesh['walk_0'=4,'walk_1'=2,'chol'=16] {'walk_0','walk_1'}, dimensions={0} | all-to-all | bytes 4194304 | tf_op jit(solution)/shard_map/all_to_all | solution.py:59
  52.7 8.5 %stack.2 = bf16[16,12,64,1024]{3,2,1,0:T(8,128)(2,1)} broadcast(bf16[12,64,1024]{2,1,0:T(8,128)(2,1)S(1)} %copy-done), dimensions={1,2,3} | broadcast | bytes 26738688 | tf_op jit(solution)/shard_map/stack | solution.py:69
  61.2 5.7 %all-to-all-start.3 = ((bf16[16,12,64,1024]{3,2,1,0:T(8,128)(2,1)}), bf16[16,12,64,1024]{3,2,1,0:T(8,128)(2,1)}, u32[]{:S(2)}, u32[]{:S(2)}) async-start(bf16[16,12,64,1024]{3,2,1,0:T(8,128)(2,1)} %stack.2), calls=%async_computation.3 | async-start | bytes 50331648 | tf_op jit(solution)/shard_map/all_to_all | solution.py:68
  66.9 0.2 convert_bitcast_fusion
  67.1 1.2 copy.38
  69.0 1.2 copy.37
  70.2 0.5 fusion
  70.7 332.6 %all-to-all-done.3 = bf16[16,12,64,1024]{3,2,1,0:T(8,128)(2,1)} async-done(((bf16[16,12,64,1024]{3,2,1,0:T(8,128)(2,1)}), bf16[16,12,64,1024]{3,2,1,0:T(8,128)(2,1)}, u32[]{:S(2)}, u32[]{:S(2)}) %all-to-all-start.3) | async-done | bytes 25165856 | tf_op jit(solution)/shard_map/all_to_all | solution.py:68
  403.3 47.7 %fusion.1 = bf16[16,8,64,1024]{3,2,1,0:T(8,128)(2,1)} fusion(bf16[16,12,64,1024]{3,2,1,0:T(8,128)(2,1)} %all-to-all-done.3, bf16[8,64,1024,1,1]{2,0,1,4,3:T(8,128)(2,1)S(1)} %bitcast.87), kind=kOutput, calls=%fused_computation.4 | convolution fusion | flops 25792872448 | bytes 42991616 | tf_op jit(solution)/shard_map/swgji,sgip->swjp/dot_general | solution.py:81
  451.0 7.3 %convert_reduce_fusion = f32[8,64,1024]{2,1,0:T(8,128)S(1)} fusion(bf16[16,8,64,1024]{3,2,1,0:T(8,128)(2,1)} %fusion.1), kind=kLoop, calls=%fused_computation.5 | loop fusion | flops 16252928 | bytes 18874368 | tf_op jit(solution)/shard_map/reduce_sum | solution.py:83
  458.4 1.2 copy.39
  459.6 0.9 multiply_reduce_fusion
  460.5 1.8 fusion.21
  462.4 4.4 copy.24
  466.8 4.5 all-to-all-start.4
  471.3 0.5 broadcast_multiply_fusion.1
  471.9 59.3 %all-to-all-done.4 = f32[8,2,64,1024]{3,2,1,0:T(8,128)} async-done(((f32[8,2,64,1024]{3,2,1,0:T(8,128)}), f32[8,2,64,1024]{3,2,1,0:T(8,128)}, u32[]{:S(2)}, u32[]{:S(2)}) %all-to-all-start.4) | async-done | bytes 4194336 | tf_op jit(solution)/shard_map/all_to_all | solution.py:93
  531.2 5.9 %fusion.16 = f32[8,64,1024]{2,0,1:T(8,128)S(1)} fusion(s32[16]{0:T(128)S(1)} %eq.84, f32[2,8,64,1024]{3,2,1,0:T(8,128)} %bitcast.37), kind=kOutput, calls=%fused_computation.12 | convolution fusion | flops 100663424 | bytes 6291520 | tf_op jit(solution)/shard_map/dot_general | solution.py:95
  537.0 2.5 copy.26
  (8 shorter events, 0.0 us)
Async XLA Ops:
  2.3 9.9 %all-to-all-start = ((s32[4,2,1,2]{3,1,2,0:T(2,128)}), s32[4,2,1,2]{3,1,2,0:T(2,128)S(1)}, u32[]{:S(2)}, u32[]{:S(2)}) async-start(s32[4,2,1,2]{3,1,2,0:T(2,128)} %bitcast), calls=%async_computation | async-start | bytes 8192 | tf_op jit(solution)/shard_map/all_to_all | solution.py:28
  24.6 28.1 %copy-start = (bf16[12,64,1024]{2,1,0:T(8,128)(2,1)S(1)}, bf16[12,64,1024]{2,1,0:T(8,128)(2,1)}, u32[]{:S(2)}) copy-start(bf16[12,64,1024]{2,1,0:T(8,128)(2,1)} %param.6) | copy-start | bytes 4718596
  61.2 5.7 %copy-start.1 = (bf16[8,64,1024]{2,1,0:T(8,128)(2,1)S(1)}, bf16[8,64,1024]{2,1,0:T(8,128)(2,1)}, u32[]{:S(2)}) copy-start(bf16[8,64,1024]{2,1,0:T(8,128)(2,1)} %param.9) | copy-start | bytes 3145732
  61.2 342.1 %all-to-all-start.3 = ((bf16[16,12,64,1024]{3,2,1,0:T(8,128)(2,1)}), bf16[16,12,64,1024]{3,2,1,0:T(8,128)(2,1)}, u32[]{:S(2)}, u32[]{:S(2)}) async-start(bf16[16,12,64,1024]{3,2,1,0:T(8,128)(2,1)} %stack.2), calls=%async_computation.3 | async-start | bytes 50331648 | tf_op jit(solution)/shard_map/all_to_all | solution.py:68
  466.8 64.4 %all-to-all-start.4 = ((f32[8,2,64,1024]{3,2,1,0:T(8,128)}), f32[8,2,64,1024]{3,2,1,0:T(8,128)}, u32[]{:S(2)}, u32[]{:S(2)}) async-start(f32[8,2,64,1024]{3,2,1,0:T(8,128)} %copy.24), calls=%async_computation.4 | async-start | bytes 8388608 | tf_op jit(solution)/shard_map/all_to_all | solution.py:93
